TPU v7x, 32 devices: a whole 2x2x4 slice. The times are simulated.
32 devices in a mesh: layer: 8 (over y, x, core), tensor: 4 (over z).
Axes of the slice: x: 2, y: 2, z: 4, core: 2. Of those that a mesh axis runs over, the one named last changes fastest.
Arguments:
- gradient: bfloat16 [8, 1024, 8192], P(None, 'tensor', 'layer'), may hold values from -8 to 8
- row_basis: bfloat16 [8, 1024, 256], P('layer', 'tensor'), may hold values from -0.1875 to 0.1875
- column_basis: bfloat16 [8, 8192, 256], P('layer', 'tensor'), may hold values from -0.0625 to 0.0625
- row_eigen: float32 [8, 256], P('layer'), may hold values from 0.01 to 10
- column_eigen: float32 [8, 256], P('layer'), may hold values from 0.01 to 10
- row_escape: float32 [8], P('layer'), may hold values from 0.02 to 0.2
- column_escape: float32 [8], P('layer'), may hold values from 0.02 to 0.2
Outputs:
- update: bfloat16 [8, 1024, 8192], P(None, 'tensor', 'layer')
All inputs are finite; a program needn't handle non-finite values.
Results may differ from a plain program's by a relative error of at most 0.0055.
Values may be sent and summed in bfloat16 or wider, within the bound.
A program may use at most 128 MiB of HBM per device.

v0:
```python
import jax
import jax.numpy as jnp
from jax import lax
from jax.sharding import PartitionSpec as P


def coefficients(row_eigen, column_eigen, row_escape, column_escape):
    row_base = row_escape ** (-0.25)
    column_base = column_escape ** (-0.25)
    row_coef = (row_eigen + row_escape[:, None]) ** (-0.25) - row_base[:, None]
    column_coef = (column_eigen + column_escape[:, None]) ** (-0.25) - column_base[:, None]
    return (row_base, column_base, row_coef, column_coef)


def group_norm(local_block):
    partial_sq = jnp.sum(jnp.square(local_block.astype(jnp.float32)), axis=(1, 2))
    return lax.psum(partial_sq, "tensor")


def finish(raw_update, grad_sq):
    update_sq = lax.psum(jnp.sum(jnp.square(raw_update), axis=(1, 2)), "tensor")
    factor = jnp.sqrt((grad_sq + 1.0) / (update_sq + 1.0))
    return (raw_update * factor[:, None, None]).astype(jnp.bfloat16)


def body(gradient, row_basis, column_basis, row_eigen, column_eigen, row_escape, column_escape):
    row_base, column_base, row_coef, column_coef = coefficients(
        row_eigen, column_eigen, row_escape, column_escape
    )
    both_base = (row_base * column_base)[:, None, None]
    group_block = lax.all_to_all(gradient, "layer", split_axis=0, concat_axis=2, tiled=True)
    grad_sq = group_norm(group_block)
    own_proj = lax.psum_scatter(
        jnp.einsum(
            "lrk,lrd->dlk", row_basis, group_block, preferred_element_type=jnp.float32
        ).astype(jnp.bfloat16),
        "tensor",
        scatter_dimension=0,
        tiled=True,
    ).astype(jnp.float32)
    scaled = (own_proj * row_coef[None]).astype(jnp.bfloat16)
    core_part = jnp.einsum("dlk,ldj->lkj", scaled, column_basis, preferred_element_type=jnp.float32)
    core_mat = lax.psum(core_part.astype(jnp.bfloat16), "tensor")
    whole_columns = lax.all_gather(column_basis, "tensor", axis=1, tiled=True)
    middle = jnp.einsum(
        "lrd,ldk->lrk", group_block, whole_columns, preferred_element_type=jnp.float32
    )
    row_term = jnp.einsum(
        "lrk,dlk->lrd",
        row_basis,
        lax.all_gather(scaled, "tensor", axis=0, tiled=True),
        preferred_element_type=jnp.float32,
    )
    mixed = row_base[:, None, None] * middle + jnp.einsum(
        "lrk,lkj->lrj", row_basis, core_mat, preferred_element_type=jnp.float32
    )
    left_factor = (mixed * column_coef[:, None, :]).astype(jnp.bfloat16)
    raw_update = both_base * group_block.astype(jnp.float32) + column_base[:, None, None] * row_term
    raw_update = raw_update + jnp.einsum(
        "lrk,ldk->lrd", left_factor, whole_columns, preferred_element_type=jnp.float32
    )
    rows_block = finish(raw_update, grad_sq)
    return lax.all_to_all(rows_block, "layer", split_axis=2, concat_axis=0, tiled=True)


def solution(mesh):
    in_specs = (
        P(None, "tensor", "layer"),
        P("layer", "tensor", None),
        P("layer", "tensor", None),
        P("layer", None),
        P("layer", None),
        P("layer"),
        P("layer"),
    )
    out_specs = P(None, "tensor", "layer")
    return jax.shard_map(body, mesh=mesh, in_specs=in_specs, out_specs=out_specs, check_vma=False)
```

profile of v0, /device:TPU:0, one launch (start us, length us, event | category | flops | bytes accessed | tf_op | source)
XLA Modules:
  0.0 558.4 jit_solution(9425964493506922182)
XLA Ops:
  6.5 54.5 %all_to_all.36 = bf16[8,256,1024]{2,1,0:T(8,128)(2,1)} all-to-all(bf16[8,256,1024]{2,1,0:T(8,128)(2,1)} %param.7), channel_id=1, replica_groups=mesh['layer'=8,'tensor'=4] {'layer'}, dimensions={0} | all-to-all | bytes 8388608 | tf_op jit(solution)/shard_map/all_to_all | solution.py:31
  61.0 6.4 %copy.15 = bf16[1,256,8,1024]{1,3,2,0:T(8,128)(2,1)} copy(bf16[1,256,8,1024]{3,1,2,0:T(8,128)(2,1)} %bitcast.80) | data formatting | bytes 8388608 | tf_op jit(solution)/shard_map/all_to_all | solution.py:31
  67.4 5.4 fusion.2
  72.9 0.7 all-gather.5.cloned.1.call-update
  74.4 75.4 %reduce-scatter.2.cloned.1.call-done = bf16[2048,1,256]{2,0,1:T(8,128)(2,1)} async-done(((bf16[8192,1,256]{2,0,1:T(8,128)(2,1)}), bf16[2048,1,256]{2,0,1:T(8,128)(2,1)}) %reduce-scatter.2.cloned.1.call-update) | async-done | bytes 1048592 | tf_op jit(solution)/shard_map/reduce_scatter | solution.py:33
  149.8 2.4 multiply_convert_fusion.1
  153.0 4.9 multiply_reduce_fusion.1
  158.0 74.7 %all-gather.5.cloned.1.call-done = bf16[1,8192,256]{2,1,0:T(8,128)(2,1)} async-done(((bf16[1,2048,256]{2,1,0:T(8,128)(2,1)}), bf16[1,8192,256]{2,1,0:T(8,128)(2,1)}) %all-gather.5.cloned.1.call-update) | async-done | bytes 4194320 | tf_op jit(solution)/shard_map/all_gather | solution.py:44
  232.7 4.8 fusion.10
  237.5 1.1 convolution_convert_fusion.1
  238.6 75.0 %all-gather.3.cloned.1.call-done = bf16[8192,1,256]{2,0,1:T(8,128)(2,1)} async-done(((bf16[2048,1,256]{2,0,1:T(8,128)(2,1)}), bf16[8192,1,256]{2,0,1:T(8,128)(2,1)}) %all-gather.3.cloned.1.call-update) | async-done | bytes 4194320 | tf_op jit(solution)/shard_map/all_gather | solution.py:51
  313.6 8.0 %fusion.1 = f32[256,8192]{0,1:T(8,128)} fusion(bf16[256,8192]{0,1:T(8,128)(2,1)} %bitcast.79, bf16[8192,1,256]{2,0,1:T(8,128)(2,1)} %all-gather.3.cloned.1.call-done, f32[]{:T(128)} %bitcast.4, f32[]{:T(128)} %bitcast, bf16[1,256,256]{2,1,0:T(8,128)(2,1)S(1)} %copy-done), kind=kOutput, calls=%fused_computation.3 | convolution fusion | flops 1082130432 | bytes 16908296 | tf_op jit(solution)/shard_map/lrk,dlk->lrd/dot_general | solution.py:48
  321.6 27.3 %all-reduce.3.cloned.1.call-done = bf16[256,256]{1,0:T(8,128)(2,1)} async-done(((bf16[256,256]{1,0:T(8,128)(2,1)}), bf16[256,256]{1,0:T(8,128)(2,1)}) %all-reduce.3.cloned.1.call-update) | async-done | bytes 131088 | tf_op jit(solution)/shard_map/psum | solution.py:43
  348.9 11.0 %multiply_reduce_fusion = (f32[]{:T(128)}, f32[256,8192]{0,1:T(8,128)}) fusion(f32[256,8192]{0,1:T(8,128)} %fusion.1, bf16[1,8192,256]{2,1,0:T(8,128)(2,1)} %all-gather.5.cloned.1.call-done, f32[256,256]{1,0:T(8,128)S(1)} %fusion.10, bf16[256,256]{1,0:T(8,128)(2,1)} %all-reduce.3.cloned.1.call-done, bf16[1,256,256]{2,1,0:T(8,128)(2,1)S(1)} %copy-done, ...), kind=kOutput, calls=%fused_computation.7 | convolution fusion | flops 1113784320 | bytes 21496836 | tf_op jit(solution)/shard_map/lrk,ldk->lrd/dot_general | solution.py:59
  359.9 11.3 %all-reduce = (f32[1]{0:T(128)}, f32[1]{0:T(128)}) all-reduce(f32[1]{0:T(128)} %bitcast.19, f32[1]{0:T(128)} %bitcast.20), channel_id=1, replica_groups=mesh['layer'=8,'tensor'=4] {'tensor'}, use_global_device_ids=true, to_apply=%region_3.0 | all-reduce | flops 2 | bytes 16 | tf_op jit(solution)/shard_map/psum | solution.py:17
  372.5 4.1 fusion.3
  376.5 49.5 %copy.24 = bf16[1,256,8192]{1,0,2:T(2,128)(2,1)} copy(bf16[1,256,8192]{1,2,0:T(8,128)(2,1)S(1)} %fusion.3) | data formatting | bytes 8388608 | tf_op jit(solution)/shard_map/convert_element_type | solution.py:23
  426.1 0.5 broadcast.23
  426.6 43.5 %reduce.4 = bf16[8192,256]{1,0:T(8,128)(2,1)} reduce(bf16[8192,1,256]{2,1,0:T(2,128)(2,1)} %bitcast.81, bf16[]{:T(256)} %broadcast.23), dimensions={1}, to_apply=%bitcast.74.reduce_sub_computation | reduce | bytes 8388610
  470.1 7.0 %reshape.90 = bf16[8,2,131072]{2,1,0:T(2,128)(2,1)} reshape(bf16[8192,256]{1,0:T(8,128)(2,1)} %reduce.4) | data formatting | bytes 8388608
  477.1 53.6 %all_to_all.37 = bf16[8,2,131072]{2,1,0:T(2,128)(2,1)} all-to-all(bf16[8,2,131072]{2,1,0:T(2,128)(2,1)} %reshape.90), channel_id=1, replica_groups=mesh['layer'=8,'tensor'=4] {'layer'}, dimensions={0} | all-to-all | bytes 8388608 | tf_op jit(solution)/shard_map/all_to_all | solution.py:63
  530.6 8.7 %reshape.91 = bf16[8192,1,256]{2,1,0:T(2,128)(2,1)} reshape(bf16[8,2,131072]{2,1,0:T(2,128)(2,1)} %all_to_all.37) | data formatting | bytes 8388608
  539.4 6.1 %copy.22 = bf16[1,256,8192]{1,2,0:T(8,128)(2,1)} copy(bf16[1,256,8192]{1,0,2:T(2,128)(2,1)} %bitcast.82) | data formatting | bytes 8388608
  545.4 6.5 %copy.19 = bf16[8,256,1024]{2,1,0:T(8,128)(2,1)} copy(bf16[8,256,1024]{1,2,0:T(8,128)(2,1)} %bitcast.83) | data formatting | bytes 8388608 | tf_op jit(solution)/shard_map/all_to_all | solution.py:63
  (21 shorter events, 0.2 us)
Async XLA Ops:
  6.5 60.9 %copy-start = (bf16[1,256,256]{2,1,0:T(8,128)(2,1)S(1)}, bf16[1,256,256]{2,1,0:T(8,128)(2,1)}, u32[]{:S(2)}) copy-start(bf16[1,256,256]{2,1,0:T(8,128)(2,1)} %param.8) | copy-start | bytes 393220
  6.5 143.3 %reduce-scatter.2.cloned.1.call-start = ((), (), s32[]{:S(2)}) async-start(), calls=%async_computation.3 | async-start | bytes 5242880 | tf_op jit(solution)/shard_map/reduce_scatter | solution.py:33
  72.8 1.5 copy-start.4
  72.8 80.2 %copy-start.5 = (f32[1,256]{1,0:T(1,128)S(1)}, f32[1,256]{1,0:T(1,128)}, u32[]{:S(2)}) copy-start(f32[1,256]{1,0:T(1,128)} %param.11) | copy-start | bytes 3076
  72.9 159.8 %all-gather.5.cloned.1.call-start = ((), (), s32[]{:S(2)}) async-start(), calls=%async_computation.5 | async-start | bytes 5242880 | tf_op jit(solution)/shard_map/all_gather | solution.py:44
  73.6 239.9 %all-gather.3.cloned.1.call-start = ((), (), s32[]{:S(2)}) async-start(), calls=%async_computation.4 | async-start | bytes 5242880 | tf_op jit(solution)/shard_map/all_gather | solution.py:51
  152.3 196.6 %all-reduce.3.cloned.1.call-start = ((), (), s32[]{:S(2)}) async-start(), calls=%async_computation.6 | async-start | bytes 262144 | tf_op jit(solution)/shard_map/psum | solution.py:43
  157.9 79.5 %copy-start.2 = (bf16[2048,1,256]{2,0,1:T(8,128)(2,1)S(1)}, bf16[2048,1,256]{2,0,1:T(8,128)(2,1)}, u32[]{:S(2)}) copy-start(bf16[2048,1,256]{2,0,1:T(8,128)(2,1)} %multiply_convert_fusion.1) | copy-start | bytes 3145732
  158.0 79.5 %copy-start.3 = (bf16[1,2048,256]{2,1,0:T(8,128)(2,1)S(1)}, bf16[1,2048,256]{2,1,0:T(8,128)(2,1)}, u32[]{:S(2)}) copy-start(bf16[1,2048,256]{2,1,0:T(8,128)(2,1)} %param.9) | copy-start | bytes 3145732
  545.4 6.5 %copy-start.1 = (bf16[1,256,256]{2,1,0:T(8,128)(2,1)S(1)}, bf16[1,256,256]{2,1,0:T(8,128)(2,1)}, u32[]{:S(2)}) copy-start(bf16[1,256,256]{2,1,0:T(8,128)(2,1)} %param.8) | copy-start | bytes 393220
Sparse Core Ops, SparseCore 0:
  73.0 76.7 reduce-scatter.1
  151.4 81.2 all-gather.4
  234.3 79.2 all-gather.2
  315.7 33.1 all-reduce.2
where the time goes:
time: 559 us; the launch traced here: 558 us
  waiting for transfers between devices  253 us (45%)
  blocking collectives  119 us (21%)
  local copies, waits for them, and re-layouts  84.7 us (15%)
  other arithmetic  54.9 us (10%)
  matrix products  30.3 us (5%)
  between operations  15.9 us (3%)
    reduce_scatter x1, waiting for transfers between devices, body(): lax.psum_scatter(jnp.einsum('lrk,lrd->dlk', row_basis, group_block, prefe...  75.4 us
    all_gather x1, waiting for transfers between devices, body(): lax.all_gather(scaled, 'tensor', axis=0, tiled=True)  75 us
    all_gather x1, waiting for transfers between devices, body(): whole_columns = lax.all_gather(column_basis, 'tensor', axis=1, tiled=True)  74.7 us
    all_to_all x1, blocking collectives, body(): lax.all_to_all(gradient, 'layer', split_axis=0, concat_axis=2, tiled=True)  54.5 us
    all_to_all x1, blocking collectives, body(): lax.all_to_all(rows_block, 'layer', split_axis=2, concat_axis=0, tiled=True)  53.6 us
    convert_element_type x1, local copies, waits for them, and re-layouts, finish(): return (raw_update * factor[:, None, None]).astype(jnp.bfloat16)  49.5 us
    unnamed x1, other arithmetic  43.5 us
    psum x1, waiting for transfers between devices, body(): core_mat = lax.psum(core_part.astype(jnp.bfloat16), 'tensor')  27.3 us
  transfers between devices with their start and end apart: 4, of which 4 were waited for; matrix products, arithmetic and copies ran while one was open for 4% of the time, Pallas kernels for 0%

commit v1 on v0

--- a/solution.py
+++ b/solution.py
@@ -60,7 +60,12 @@
         "lrk,ldk->lrd", left_factor, whole_columns, preferred_element_type=jnp.float32
     )
     rows_block = finish(raw_update, grad_sq)
-    return lax.all_to_all(rows_block, "layer", split_axis=2, concat_axis=0, tiled=True)
+    return jnp.concatenate(
+        lax.all_to_all(
+            jnp.stack(jnp.split(rows_block, lax.axis_size("layer"), axis=2)), "layer", 0, 0
+        ),
+        axis=0,
+    )
 
 
 def solution(mesh):

time: 559 us -> 443 us (0.79)
  local copies, waits for them, and re-layouts: 84.7 us -> 13.2 us
  other arithmetic: 54.9 us -> 11.5 us
    convert_element_type x1 -> x0, local copies, waits for them, and re-layouts: 49.5 us -> none  [finish(): return (raw_update * factor[:, None, None]).astype(jnp.bfloat16)]
    unnamed x1 -> x0, other arithmetic: 43.5 us -> none
    unnamed x16 -> x17, local copies, waits for them, and re-layouts: 22.3 us -> 0.27 us
    all_to_all x1 -> x0, local copies, waits for them, and re-layouts: 6.46 us -> none  [body(): lax.all_to_all(rows_block, 'layer', split_axis=2, concat_axis=0, tiled=True)]
    reshape x0 -> x1, local copies, waits for them, and re-layouts: none -> 6.43 us  [body(): jnp.concatenate(lax.all_to_all(jnp.stack(jnp.split(rows_block, lax.axis_s...]
  transfers between devices with their start and end apart: 4 -> 4, of which waited for: 4 -> 4; matrix products, arithmetic and copies ran while one was open for 4% -> 5% of each run, Pallas kernels for 0% -> 0%
where the time goes in v1:
time: 443 us; the launch traced here: 442 us
  waiting for transfers between devices  253 us (57%)
  blocking collectives  118 us (27%)
  matrix products  30.3 us (7%)
  between operations  16.1 us (4%)
  local copies, waits for them, and re-layouts  13.2 us (3%)
  other arithmetic  11.5 us (3%)
    reduce_scatter x1, waiting for transfers between devices, body(): lax.psum_scatter(jnp.einsum('lrk,lrd->dlk', row_basis, group_block, prefe...  75.4 us
    all_gather x1, waiting for transfers between devices, body(): lax.all_gather(scaled, 'tensor', axis=0, tiled=True)  75 us
    all_gather x1, waiting for transfers between devices, body(): whole_columns = lax.all_gather(column_basis, 'tensor', axis=1, tiled=True)  74.6 us
    all_to_all x1, blocking collectives, body(): lax.all_to_all(gradient, 'layer', split_axis=0, concat_axis=2, tiled=True)  54.5 us
    all_to_all x1, blocking collectives, body(): lax.all_to_all(jnp.stack(jnp.split(rows_block, lax.axis_size('layer'), ax...  52.6 us
    psum x1, waiting for transfers between devices, body(): core_mat = lax.psum(core_part.astype(jnp.bfloat16), 'tensor')  27.3 us
    psum x1, blocking collectives, group_norm(): return lax.psum(partial_sq, 'tensor')  11.2 us
    dot_general x1, matrix products, body(): jnp.einsum('lrk,ldk->lrd', left_factor, whole_columns, preferred_element_...  11 us
  transfers between devices with their start and end apart: 4, of which 4 were waited for; matrix products, arithmetic and copies ran while one was open for 5% of the time, Pallas kernels for 0%

profile of v1, /device:TPU:0, one launch (start us, length us, event | category | flops | bytes accessed | tf_op | source)
XLA Modules:
  0.0 442.3 jit_solution(13179299295354182582)
XLA Ops:
  6.5 54.5 %all_to_all.23 = bf16[8,256,1024]{2,1,0:T(8,128)(2,1)} all-to-all(bf16[8,256,1024]{2,1,0:T(8,128)(2,1)} %param.7), channel_id=1, replica_groups=mesh['layer'=8,'tensor'=4] {'layer'}, dimensions={0} | all-to-all | bytes 8388608 | tf_op jit(solution)/shard_map/all_to_all | solution.py:31
  61.0 6.4 %copy.8 = bf16[1,256,8,1024]{1,3,2,0:T(8,128)(2,1)} copy(bf16[1,256,8,1024]{3,1,2,0:T(8,128)(2,1)} %bitcast.104) | data formatting | bytes 8388608 | tf_op jit(solution)/shard_map/all_to_all | solution.py:31
  67.4 5.4 %fusion.2 = bf16[8192,1,256]{2,0,1:T(8,128)(2,1)} fusion(bf16[256,8192]{0,1:T(8,128)(2,1)} %bitcast.101, bf16[1,256,256]{2,1,0:T(8,128)(2,1)S(1)} %copy-done), kind=kOutput, calls=%fused_computation.5 | convolution fusion | flops 1075838976 | bytes 8519680 | tf_op jit(solution)/shard_map/lrk,lrd->dlk/dot_general | solution.py:34
  72.8 0.0 reduce-scatter.2.cloned.1.call-update
  72.9 0.0 all-gather.5.cloned.1.call-start
  72.9 0.7 all-gather.5.cloned.1.call-update
  73.6 0.0 all-gather.3.cloned.1.call-start
  74.4 75.4 %reduce-scatter.2.cloned.1.call-done = bf16[2048,1,256]{2,0,1:T(8,128)(2,1)} async-done(((bf16[8192,1,256]{2,0,1:T(8,128)(2,1)}), bf16[2048,1,256]{2,0,1:T(8,128)(2,1)}) %reduce-scatter.2.cloned.1.call-update) | async-done | bytes 1048592 | tf_op jit(solution)/shard_map/reduce_scatter | solution.py:33
  149.8 2.4 multiply_convert_fusion.1
  152.2 0.0 all-gather.3.cloned.1.call-update
  152.3 0.0 all-reduce.3.cloned.1.call-start
  153.0 5.0 %multiply_reduce_fusion.1 = f32[]{:T(128)} fusion(bf16[8,256,1024]{2,1,0:T(8,128)(2,1)} %all_to_all.23), kind=kLoop, calls=%fused_computation.8 | loop fusion | flops 6291455 | bytes 4194308 | tf_op jit(solution)/shard_map/reduce_sum | solution.py:16
  158.1 74.6 %all-gather.5.cloned.1.call-done = bf16[1,8192,256]{2,1,0:T(8,128)(2,1)} async-done(((bf16[1,2048,256]{2,1,0:T(8,128)(2,1)}), bf16[1,8192,256]{2,1,0:T(8,128)(2,1)}) %all-gather.5.cloned.1.call-update) | async-done | bytes 4194320 | tf_op jit(solution)/shard_map/all_gather | solution.py:44
  232.7 4.8 %fusion.10 = f32[256,256]{1,0:T(8,128)S(1)} fusion(bf16[256,8192]{0,1:T(8,128)(2,1)} %bitcast.102, bf16[1,8192,256]{2,1,0:T(8,128)(2,1)} %all-gather.5.cloned.1.call-done, f32[]{:T(128)} %bitcast.8), kind=kOutput, calls=%fused_computation.18 | convolution fusion | flops 1073807360 | bytes 8650756 | tf_op jit(solution)/shard_map/lrd,ldk->lrk/dot_general | solution.py:45
  237.4 1.1 convolution_convert_fusion.1
  238.6 0.0 all-reduce.3.cloned.1.call-update
  238.6 75.0 %all-gather.3.cloned.1.call-done = bf16[8192,1,256]{2,0,1:T(8,128)(2,1)} async-done(((bf16[2048,1,256]{2,0,1:T(8,128)(2,1)}), bf16[8192,1,256]{2,0,1:T(8,128)(2,1)}) %all-gather.3.cloned.1.call-update) | async-done | bytes 4194320 | tf_op jit(solution)/shard_map/all_gather | solution.py:51
  313.6 8.0 %fusion.1 = f32[256,8192]{0,1:T(8,128)} fusion(bf16[256,8192]{0,1:T(8,128)(2,1)} %bitcast.103, bf16[8192,1,256]{2,0,1:T(8,128)(2,1)} %all-gather.3.cloned.1.call-done, f32[]{:T(128)} %bitcast.4, f32[]{:T(128)} %bitcast, bf16[1,256,256]{2,1,0:T(8,128)(2,1)S(1)} %copy-done), kind=kOutput, calls=%fused_computation.3 | convolution fusion | flops 1082130432 | bytes 16908296 | tf_op jit(solution)/shard_map/lrk,dlk->lrd/dot_general | solution.py:48
  321.6 27.3 %all-reduce.3.cloned.1.call-done = bf16[256,256]{1,0:T(8,128)(2,1)} async-done(((bf16[256,256]{1,0:T(8,128)(2,1)}), bf16[256,256]{1,0:T(8,128)(2,1)}) %all-reduce.3.cloned.1.call-update) | async-done | bytes 131088 | tf_op jit(solution)/shard_map/psum | solution.py:43
  348.9 11.0 %multiply_reduce_fusion = (f32[]{:T(128)}, f32[256,8192]{0,1:T(8,128)}) fusion(f32[256,8192]{0,1:T(8,128)} %fusion.1, bf16[1,8192,256]{2,1,0:T(8,128)(2,1)} %all-gather.5.cloned.1.call-done, f32[256,256]{1,0:T(8,128)S(1)} %fusion.10, bf16[256,256]{1,0:T(8,128)(2,1)} %all-reduce.3.cloned.1.call-done, bf16[1,256,256]{2,1,0:T(8,128)(2,1)S(1)} %copy-done, ...), kind=kOutput, calls=%fused_computation.7 | convolution fusion | flops 1113784320 | bytes 21496836 | tf_op jit(solution)/shard_map/lrk,ldk->lrd/dot_general | solution.py:59
  359.9 11.2 %all-reduce = (f32[1]{0:T(128)}, f32[1]{0:T(128)}) all-reduce(f32[1]{0:T(128)} %bitcast.19, f32[1]{0:T(128)} %bitcast.20), channel_id=1, replica_groups=mesh['layer'=8,'tensor'=4] {'tensor'}, use_global_device_ids=true, to_apply=%region_3.0 | all-reduce | flops 2 | bytes 16 | tf_op jit(solution)/shard_map/psum | solution.py:17
  372.4 4.1 fusion.3
  376.8 52.6 %all_to_all.24 = bf16[8,1,256,1024]{2,3,1,0:T(8,128)(2,1)} all-to-all(bf16[8,1,256,1024]{2,3,1,0:T(8,128)(2,1)S(1)} %fusion.16), channel_id=1, replica_groups=mesh['layer'=8,'tensor'=4] {'layer'}, dimensions={0} | all-to-all | bytes 8388608 | tf_op jit(solution)/shard_map/all_to_all | solution.py:64
  429.4 6.4 %copy.10 = bf16[8,256,1024]{2,1,0:T(8,128)(2,1)} copy(bf16[8,256,1024]{1,2,0:T(8,128)(2,1)} %bitcast.105) | data formatting | bytes 8388608 | tf_op jit(solution)/shard_map/reshape | solution.py:63
  (21 shorter events, 0.3 us)
Async XLA Ops:
  6.5 60.9 %copy-start = (bf16[1,256,256]{2,1,0:T(8,128)(2,1)S(1)}, bf16[1,256,256]{2,1,0:T(8,128)(2,1)}, u32[]{:S(2)}) copy-start(bf16[1,256,256]{2,1,0:T(8,128)(2,1)} %param.8) | copy-start | bytes 393220
  6.5 143.3 %reduce-scatter.2.cloned.1.call-start = ((), (), s32[]{:S(2)}) async-start(), calls=%async_computation.3 | async-start | bytes 5242880 | tf_op jit(solution)/shard_map/reduce_scatter | solution.py:33
  72.8 1.5 copy-start.3
  72.8 80.2 %copy-start.4 = (f32[1,256]{1,0:T(1,128)S(1)}, f32[1,256]{1,0:T(1,128)}, u32[]{:S(2)}) copy-start(f32[1,256]{1,0:T(1,128)} %param.11) | copy-start | bytes 3076
  72.9 159.8 %all-gather.5.cloned.1.call-start = ((), (), s32[]{:S(2)}) async-start(), calls=%async_computation.5 | async-start | bytes 5242880 | tf_op jit(solution)/shard_map/all_gather | solution.py:44
  73.6 239.9 %all-gather.3.cloned.1.call-start = ((), (), s32[]{:S(2)}) async-start(), calls=%async_computation.4 | async-start | bytes 5242880 | tf_op jit(solution)/shard_map/all_gather | solution.py:51
  152.3 196.6 %all-reduce.3.cloned.1.call-start = ((), (), s32[]{:S(2)}) async-start(), calls=%async_computation.6 | async-start | bytes 262144 | tf_op jit(solution)/shard_map/psum | solution.py:43
  158.1 79.4 %copy-start.1 = (bf16[2048,1,256]{2,0,1:T(8,128)(2,1)S(1)}, bf16[2048,1,256]{2,0,1:T(8,128)(2,1)}, u32[]{:S(2)}) copy-start(bf16[2048,1,256]{2,0,1:T(8,128)(2,1)} %multiply_convert_fusion.1) | copy-start | bytes 3145732
  158.1 79.4 %copy-start.2 = (bf16[1,2048,256]{2,1,0:T(8,128)(2,1)S(1)}, bf16[1,2048,256]{2,1,0:T(8,128)(2,1)}, u32[]{:S(2)}) copy-start(bf16[1,2048,256]{2,1,0:T(8,128)(2,1)} %param.9) | copy-start | bytes 3145732
Sparse Core Ops, SparseCore 0:
  73.0 76.7 reduce-scatter.1
  151.4 81.2 all-gather.4
  234.2 79.2 all-gather.2
  315.7 33.1 all-reduce.2
